TPU v7x, 32 devices: a whole 2x2x4 slice. The times are simulated.
32 devices in a mesh: task: 2 (over core), row: 16 (over z, y, x).
Axes of the slice: x: 2, y: 2, z: 4, core: 2. Of those that a mesh axis runs over, the one named last changes fastest.
Arguments:
- activation_grams: float32 [2, 7168, 7168], P('task', 'row'), may hold values from -240 to 240, as said below
- adjusted_weights: bfloat16 [2, 7168, 2048], P('task', 'row'), may hold values from -0.59765625 to 0.59765625
Outputs:
- reduced_gram: float32 [7168, 7168], P('row')
- reduced_rhs: float32 [7168, 2048], P('row')
Inputs may be any that keep to these rules, and one draw needn't show every extreme that they name: Each activation_grams[m] is symmetric and positive definite.
All inputs are finite; a program needn't handle non-finite values.
Results may differ from a plain program's by a relative error of at most 0.0003.
Values may be sent and summed in bfloat16 or wider, within the bound.
A program may use at most 192 MiB of HBM per device.

v0:
```python
import jax
import jax.numpy as jnp
from jax import lax
from jax.sharding import PartitionSpec as P

PANEL_STEPS = 2


def broadcast(value, axis, source):
    kept = jnp.where(lax.axis_index(axis) == source, value, 0).astype(value.dtype)
    return lax.psum(kept, axis)


def product(left, right):
    return jnp.dot(left, right, precision=lax.Precision.HIGHEST)


def per_device(activation_grams, adjusted_weights):
    local_models, rows, width = activation_grams.shape
    columns = adjusted_weights.shape[2]
    position = lax.axis_index("row")
    start_col = position * rows
    own_block = lax.dynamic_slice_in_dim(activation_grams, start_col, rows, 2)
    diagonal_entries = jnp.diagonal(own_block, axis1=1, axis2=2)
    total_trace = lax.psum(jnp.sum(diagonal_entries, axis=1), "row")
    scaling = width / total_trace
    identity_block = jnp.eye(rows, dtype=jnp.float32)
    new_block = 0.9 * own_block + 0.1 * (diagonal_entries[:, :, None] * identity_block)
    regular = lax.dynamic_update_slice_in_dim(0.9 * activation_grams, new_block, start_col, 2)
    source = scaling[:, None, None] * regular
    form = "mbn,mnd->bd"
    initial = jnp.zeros((rows, columns), jnp.float32)
    piece = lax.all_gather(adjusted_weights, "row", axis=1, tiled=True)
    chosen = lax.slice_in_dim(source, 0, piece.shape[1], axis=2)
    folded = initial + jnp.einsum(
        form, chosen, piece.astype(jnp.float32), precision=lax.Precision.HIGHEST
    )
    merged_part = jnp.sum(source, axis=0)
    merged_rows, rhs_rows = lax.psum((merged_part, folded), "task")
    for panel in range(PANEL_STEPS):
        diag_block = lax.dynamic_slice_in_dim(merged_rows, start_col, rows, 1)
        diag_block = jnp.where(position >= panel, diag_block, identity_block)
        factor = jnp.linalg.cholesky(diag_block)
        upper_rows = jax.scipy.linalg.solve_triangular(factor, merged_rows, lower=True)
        solved_rows = jax.scipy.linalg.solve_triangular(factor, rhs_rows, lower=True)
        upper_rows, solved_rows = (
            broadcast(upper_rows, "row", panel),
            broadcast(solved_rows, "row", panel),
        )
        mine = lax.dynamic_slice_in_dim(upper_rows, start_col, rows, 1).T
        merged_next = merged_rows - product(mine, upper_rows)
        rhs_next = rhs_rows - product(mine, solved_rows)
        merged_rows = jnp.where(
            position == panel, upper_rows, jnp.where(position > panel, merged_next, merged_rows)
        )
        rhs_rows = jnp.where(
            position == panel, solved_rows, jnp.where(position > panel, rhs_next, rhs_rows)
        )
    return (merged_rows, rhs_rows)


def solution(mesh):
    placed = (P("task", "row", None), P("task", "row", None))
    return jax.shard_map(
        per_device,
        mesh=mesh,
        in_specs=placed,
        out_specs=(P("row", None), P("row", None)),
        check_vma=False,
    )
```

profile of v0, /device:TPU:0, one launch (start us, length us, event | category | flops | bytes accessed | tf_op | source)
XLA Modules:
  0.0 1975.7 jit_solution(9161190287944961805)
XLA Ops:
  7.9 14.6 copy.34
  23.9 3.9 gather_fusion
  28.5 45.8 %psum.49 = f32[1]{0:T(128)} all-reduce(f32[1]{0:T(128)} %bitcast.2), channel_id=1, replica_groups=mesh['task'=2,'row'=16] {'row'}, use_global_device_ids=true, to_apply=%region_1.2 | all-reduce | flops 1 | bytes 8 | tf_op jit(solution)/shard_map/psum | solution.py:25
  75.0 12.2 broadcast_multiply_fusion
  87.1 2.3 add_dynamic-update-slice_fusion
  89.4 12.3 multiply_bitcast_fusion
  101.7 222.6 %all-gather.2.cloned.1.call-done = bf16[1,7168,2048]{2,1,0:T(8,128)(2,1)} async-done(((bf16[1,448,2048]{2,1,0:T(8,128)(2,1)}), bf16[1,7168,2048]{2,1,0:T(8,128)(2,1)}) %all-gather.2.cloned.1.call-update) | async-done | bytes 29360144 | tf_op jit(solution)/shard_map/all_gather | solution.py:33
  324.3 47.4 %fusion = f32[448,2048]{1,0:T(8,128)} fusion(f32[448,7168]{0,1:T(8,128)} %multiply_bitcast_fusion, bf16[1,7168,2048]{2,1,0:T(8,128)(2,1)} %all-gather.2.cloned.1.call-done), kind=kOutput, calls=%fused_computation.5 | convolution fusion | flops 78920024064 | bytes 45875200 | tf_op jit(solution)/shard_map/mbn,mnd->bd/dot_general | solution.py:35
  372.0 61.9 %all-reduce.16.cloned.1.call-done = (f32[448,7168]{0,1:T(8,128)}, f32[448,2048]{1,0:T(8,128)}) async-done(((f32[448,7168]{0,1:T(8,128)}, f32[448,2048]{1,0:T(8,128)}), (f32[448,7168]{0,1:T(8,128)}, f32[448,2048]{1,0:T(8,128)})) %all-reduce.16.cloned.1.call-update) | async-done | bytes 16515088 | tf_op jit(solution)/shard_map/psum | solution.py:39
  437.0 11.7 cholesky.292
  448.8 9.8 custom-call.33
  459.3 11.7 cholesky.311
  471.0 10.2 custom-call.34
  481.8 11.7 cholesky.332
  494.2 9.8 custom-call.35
  505.3 5.8 cholesky.352
  516.1 9.0 while.8
  516.8 2.3 bitcast_dynamic-update-slice_fusion.4
  519.7 2.3 bitcast_dynamic-update-slice_fusion.4
  522.7 2.3 bitcast_dynamic-update-slice_fusion.4
  525.2 39.5 %custom-call.36 = f32[4,128,128]{1,2,0:T(8,128)S(1)} custom-call(f32[4,128,128]{2,1,0:T(8,128)S(1)} %pad_maximum_fusion), custom_call_target="InvertDiagBlocksLowerTriangular" | custom-call | tf_op jit(solution)/shard_map/jit(_solve_triangular)/triangular_solve | solution.py:44
  564.7 5.7 fusion.32
  570.5 9.4 convolution_subtract_fusion.3
  579.9 3.8 fusion.105
  583.7 12.8 convolution_subtract_fusion.2
  596.6 5.2 fusion.107
  601.7 21.1 %fusion.19 = f32[64,7168]{0,1:T(8,128)} fusion(f32[128,7168]{1,0:T(8,128)} %fusion.107, f32[128,7168]{1,0:T(8,128)} %copy-done.3, f32[128,7168]{1,0:T(8,128)S(1)} %fusion.32, f32[448,7168]{0,1:T(8,128)S(1)} %bitcast.150, f32[448,448]{1,0:T(8,128)S(1)} %copy-done.18), kind=kOutput, calls=%fused_computation.31 | convolution fusion | flops 2119892992 | bytes 16613376 | tf_op jit(solution)/shard_map/jit(_solve_triangular)/triangular_solve | solution.py:44
  622.9 5.3 copy.43
  628.1 5.2 copy.42
  633.4 5.4 copy.41
  638.8 2.3 fusion.60
  641.0 2.2 convolution_subtract_fusion.7
  644.3 2.5 convolution_subtract_fusion.5
  647.9 3.1 fusion.49
  651.6 3.5 fusion.119
  659.6 5.7 maximum_select_fusion
  665.4 488.1 %all-reduce.14.cloned.1.call-done = (f32[448,7168]{0,1:T(8,128)}, f32[448,2048]{1,0:T(8,128)}) async-done(((f32[448,7168]{0,1:T(8,128)}, f32[448,2048]{1,0:T(8,128)}), (f32[448,7168]{0,1:T(8,128)}, f32[448,2048]{1,0:T(8,128)})) %all-reduce.14.cloned.1.call-update) | async-done | bytes 16515088 | tf_op jit(solution)/shard_map/psum | solution.py:11
  1153.5 33.6 %fusion.2 = f32[448,7168]{0,1:T(8,128)S(1)} fusion(f32[448,7168]{0,1:T(8,128)} %get-tuple-element.61, f32[448,7168]{0,1:T(8,128)} %get-tuple-element.63, pred[]{:T(512)S(6)} %gt.8, pred[]{:T(512)S(6)} %eq.27, s32[]{:T(128)S(6)} %select_n.105), kind=kOutput, calls=%fused_computation.9 | convolution fusion | flops 17273389056 | bytes 57802760 | tf_op jit(solution)/shard_map/dot_general | solution.py:15
  1187.1 5.2 copy-done
  1194.1 11.7 cholesky.368
  1206.0 9.8 custom-call.37
  1216.4 11.7 cholesky.387
  1229.5 10.0 custom-call.38
  1240.0 11.7 cholesky.408
  1252.5 9.8 custom-call.39
  1263.5 5.8 cholesky.428
  1273.6 8.5 while.9
  1282.2 39.5 %custom-call.40 = f32[4,128,128]{1,2,0:T(8,128)S(1)} custom-call(f32[4,128,128]{2,1,0:T(8,128)S(1)} %pad_maximum_fusion.1), custom_call_target="InvertDiagBlocksLowerTriangular" | custom-call | tf_op jit(solution)/shard_map/jit(_solve_triangular)/triangular_solve | solution.py:44
  1321.8 5.7 fusion.30
  1327.6 9.4 convolution_subtract_fusion.1
  1337.0 4.1 fusion.109
  1341.1 12.5 convolution_subtract_fusion
  1353.6 5.2 fusion.111
  1358.8 21.1 %fusion.16 = f32[64,7168]{0,1:T(8,128)} fusion(f32[128,7168]{1,0:T(8,128)} %fusion.111, f32[128,7168]{1,0:T(8,128)} %copy-done.4, f32[128,7168]{1,0:T(8,128)S(1)} %fusion.30, f32[448,7168]{0,1:T(8,128)S(1)} %bitcast.148, f32[448,448]{1,0:T(8,128)S(1)} %copy-done.16), kind=kOutput, calls=%fused_computation.30 | convolution fusion | flops 2119892992 | bytes 16613376 | tf_op jit(solution)/shard_map/jit(_solve_triangular)/triangular_solve | solution.py:44
  1379.9 5.3 copy.52
  1385.2 5.2 copy.51
  1390.4 5.2 copy.50
  1395.7 10.0 fusion.28
  1413.8 3.5 fusion.121
  1421.7 5.7 maximum_select_fusion.1
  1427.5 483.9 %all-reduce.12.cloned.1.call-done = (f32[448,7168]{0,1:T(8,128)}, f32[448,2048]{1,0:T(8,128)}) async-done(((f32[448,7168]{0,1:T(8,128)}, f32[448,2048]{1,0:T(8,128)}), (f32[448,7168]{0,1:T(8,128)}, f32[448,2048]{1,0:T(8,128)})) %all-reduce.12.cloned.1.call-update) | async-done | bytes 16515088 | tf_op jit(solution)/shard_map/psum | solution.py:11
  1911.4 33.6 %fusion.3 = f32[448,7168]{0,1:T(8,128)} fusion(f32[448,7168]{0,1:T(8,128)} %get-tuple-element.59, f32[448,7168]{0,1:T(8,128)} %copy-done, pred[]{:T(512)S(6)} %gt.9, pred[]{:T(512)S(6)} %eq.26, s32[]{:T(128)S(6)} %select_n.105), kind=kOutput, calls=%fused_computation.10 | convolution fusion | flops 17273389056 | bytes 57802760 | tf_op jit(solution)/shard_map/dot_general | solution.py:15
  1945.1 9.1 fusion.29
  1954.2 14.6 copy.55
  (154 shorter events, 50.2 us)
Async XLA Ops:
  7.2 317.2 %all-gather.2.cloned.1.call-start = ((), (), s32[]{:S(2)}) async-start(), calls=%async_computation | async-start | bytes 31195136 | tf_op jit(solution)/shard_map/all_gather | solution.py:33
  7.9 426.0 %all-reduce.16.cloned.1.call-start = ((), (), s32[]{:S(2)}) async-start(), calls=%async_computation.3 | async-start | bytes 36700160 | tf_op jit(solution)/shard_map/psum | solution.py:39
  371.7 781.8 %all-reduce.14.cloned.1.call-start = ((), (), s32[]{:S(2)}) async-start(), calls=%async_computation.2 | async-start | bytes 36700160 | tf_op jit(solution)/shard_map/psum | solution.py:11
  436.9 44.8 %copy-start.21 = (f32[448,448]{1,0:T(8,128)}, f32[448,448]{1,0:T(8,128)S(1)}, u32[]{:S(2)}) copy-start(f32[448,448]{1,0:T(8,128)S(1)} %fusion.63) | copy-start | bytes 2408452
  493.5 90.2 %slice-start.4 = ((s8[14680064]{0:T(1024)(128)(4,1)}), s8[2097152]{0:T(1024)(128)(4,1)S(1)}, s32[]{:S(2)}) async-start(s8[14680064]{0:T(1024)(128)(4,1)} %bitcast.149), calls=%async_computation.8 | async-start | bytes 4194304
  515.2 0.9 copy-start.17
  564.7 5.8 copy-start.18
  564.7 19.0 slice-start.5
  570.4 31.3 %copy-start.1 = (f32[128,7168]{1,0:T(8,128)}, f32[128,7168]{1,0:T(8,128)S(1)}, u32[]{:S(2)}) copy-start(f32[128,7168]{1,0:T(8,128)S(1)} %fusion.32) | copy-start | bytes 11010052
  570.5 13.3 slice-start.6
  570.5 13.3 slice-start.7
  583.7 12.8 copy-start.3
  646.8 4.8 copy-start.14
  651.6 5.6 copy-start.13
  655.1 3.4 copy-start.10
  655.1 4.5 copy-start.12
  665.4 1246.1 %all-reduce.12.cloned.1.call-start = ((), (), s32[]{:S(2)}) async-start(), calls=%async_computation.1 | async-start | bytes 36700160 | tf_op jit(solution)/shard_map/psum | solution.py:11
  1187.1 5.2 copy-start
  1194.1 57.6 %copy-start.20 = (f32[448,448]{1,0:T(8,128)}, f32[448,448]{1,0:T(8,128)S(1)}, u32[]{:S(2)}) copy-start(f32[448,448]{1,0:T(8,128)S(1)} %fusion.62) | copy-start | bytes 2408452
  1251.8 89.3 %slice-start = ((s8[14680064]{0:T(1024)(128)(4,1)}), s8[2097152]{0:T(1024)(128)(4,1)S(1)}, s32[]{:S(2)}) async-start(s8[14680064]{0:T(1024)(128)(4,1)} %bitcast.147), calls=%async_computation.4 | async-start | bytes 4194304
  1272.7 0.9 copy-start.15
  1321.8 5.8 copy-start.16
  1321.8 19.3 slice-start.1
  1327.5 31.2 %copy-start.2 = (f32[128,7168]{1,0:T(8,128)}, f32[128,7168]{1,0:T(8,128)S(1)}, u32[]{:S(2)}) copy-start(f32[128,7168]{1,0:T(8,128)S(1)} %fusion.30) | copy-start | bytes 11010052
  1327.6 13.5 slice-start.2
  1327.6 13.5 slice-start.3
  1341.1 12.5 copy-start.4
  1405.7 5.5 copy-start.5
  1410.0 3.7 copy-start.11
  1413.8 5.6 copy-start.9
  1417.2 3.4 copy-start.7
  1417.2 4.5 copy-start.8
  1911.4 33.6 %copy-start.6 = (f32[448,2048]{1,0:T(8,128)S(1)}, f32[448,2048]{1,0:T(8,128)}, u32[]{:S(2)}) copy-start(f32[448,2048]{1,0:T(8,128)} %copy-done.5) | copy-start | bytes 11010052
  1911.4 33.6 %copy-start.19 = (f32[448,2048]{1,0:T(8,128)S(1)}, f32[448,2048]{1,0:T(8,128)}, u32[]{:S(2)}) copy-start(f32[448,2048]{1,0:T(8,128)} %get-tuple-element.60) | copy-start | bytes 11010052
Sparse Core Ops, SparseCore 0:
  10.7 313.5 all-gather.1
  371.9 62.0 all-reduce.15
  665.5 487.9 all-reduce.13
  1427.6 483.7 all-reduce.11
where the time goes:
time: 1980 us
  waiting for transfers between devices  1260 us (64%)
  matrix products  282 us (14%)
  other arithmetic  273 us (14%)
  local copies, waits for them, and re-layouts  96.1 us (5%)
  blocking collectives  45.8 us (2%)
  between operations  21.1 us (1%)
    psum x2, waiting for transfers between devices, broadcast(): return lax.psum(kept, axis)  972 us
    all_gather x1, waiting for transfers between devices, per_device(): piece = lax.all_gather(adjusted_weights, 'row', axis=1, tiled=True)  223 us
    another operation x29, other arithmetic, per_device(): factor = jnp.linalg.cholesky(diag_block)  146 us
    another operation x14, matrix products, per_device(): jax.scipy.linalg.solve_triangular(factor, merged_rows, lower=True)  123 us
    dot_general x4, matrix products, product(): return jnp.dot(left, right, precision=lax.Precision.HIGHEST)  86.3 us
    another operation x11, other arithmetic, per_device(): jax.scipy.linalg.solve_triangular(factor, merged_rows, lower=True)  79.5 us
    psum x1, waiting for transfers between devices, per_device(): merged_rows, rhs_rows = lax.psum((merged_part, folded), 'task')  61.9 us
    another operation x29, local copies, waits for them, and re-layouts, per_device(): jax.scipy.linalg.solve_triangular(factor, merged_rows, lower=True)  49 us
  transfers between devices with their start and end apart: 4, of which 4 were waited for; matrix products, arithmetic and copies ran while one was open for 2% of the time, Pallas kernels for 0%

commit v1 on v0

v1 whole, which is shorter than its diff:
```python
import jax
import jax.numpy as jnp
from jax import lax
from jax.sharding import PartitionSpec as P

PANEL_STEPS = 2


def product(left, right):
    return jnp.dot(left, right, precision=lax.Precision.HIGHEST)


def inverse_of(factor):
    identity = jnp.eye(factor.shape[0], dtype=factor.dtype)
    return jax.scipy.linalg.solve_triangular(factor, identity, lower=True)


def leading_block(columns_block, parts, rows, wide):
    position = lax.axis_index("row")
    holders = wide // rows
    if rows % parts == 0:
        pieces = lax.all_to_all(
            columns_block.reshape(parts, rows // parts, wide), "row", 0, 0, tiled=True
        )[:holders]
        gathered = lax.all_gather(pieces, "row", axis=1, tiled=True)
        return gathered.reshape(wide, wide)
    placed = jnp.zeros((wide, wide), columns_block.dtype)
    kept = jnp.where(position < holders, columns_block, 0)
    start = jnp.minimum(position, holders - 1) * rows
    return lax.psum(lax.dynamic_update_slice_in_dim(placed, kept, start, 0), "row")


def per_device(parts, activation_grams, adjusted_weights):
    gram = activation_grams[0]
    rows, width = gram.shape
    columns = adjusted_weights.shape[2]
    wide = PANEL_STEPS * rows
    position = lax.axis_index("row")
    task = lax.axis_index("task")
    start_col = position * rows
    weights = lax.all_gather(adjusted_weights[0], "row", axis=0, tiled=True)

    own_block = lax.dynamic_slice_in_dim(gram, start_col, rows, 1)
    diagonal_entries = jnp.diagonal(own_block)
    scaling = width / lax.psum(jnp.sum(diagonal_entries), "row")
    row_ids = lax.broadcasted_iota(jnp.int32, (rows, width), 0) + start_col
    col_ids = lax.broadcasted_iota(jnp.int32, (rows, width), 1)
    source = scaling * (0.9 * gram + jnp.where(row_ids == col_ids, 0.1 * gram, 0.0))

    panel_cols = lax.psum(source[:, :wide], "task")
    corner = leading_block(panel_cols, parts, rows, wide)
    first_inverse = inverse_of(jnp.linalg.cholesky(corner[:rows, :rows]))
    left = product(corner[rows:, :rows], first_inverse.T)
    second = jnp.linalg.cholesky(corner[rows:, rows:] - product(left, left.T))
    second_inverse = inverse_of(second)
    coupling = -product(second_inverse, product(left, first_inverse))
    solver = jnp.where(
        task == 0,
        jnp.concatenate([first_inverse, jnp.zeros_like(first_inverse)], axis=1),
        jnp.concatenate([coupling, second_inverse], axis=1),
    )
    mine = product(solver, panel_cols.T)
    upper = lax.all_gather(mine, "row", axis=1, tiled=True)

    high = lax.reduce_precision(source, 8, 7)
    low = (source - high).astype(jnp.bfloat16)
    folded = jnp.dot(
        high.astype(jnp.bfloat16), weights, preferred_element_type=jnp.float32
    ) + jnp.dot(low, weights, preferred_element_type=jnp.float32)

    pieces = lax.all_to_all(folded, "row", 1, 0, tiled=True)
    held, solver = lax.optimization_barrier((pieces[:wide], solver))
    top = lax.psum(held, "task")
    solved = lax.all_gather(product(solver, top), "row", axis=1, tiled=True)

    below = position >= PANEL_STEPS
    holds = position == task
    merged_part = jnp.where(
        below, source - product(mine.T, upper), jnp.where(holds, upper, 0.0)
    )
    rhs_part = jnp.where(
        below, folded - product(mine.T, solved), jnp.where(holds, solved, 0.0)
    )
    return lax.psum((merged_part, rhs_part), "task")


def solution(mesh):
    assert mesh.shape["task"] == PANEL_STEPS
    parts = mesh.shape["row"]
    placed = (P("task", "row", None), P("task", "row", None))
    return jax.shard_map(
        lambda grams, weights: per_device(parts, grams, weights),
        mesh=mesh,
        in_specs=placed,
        out_specs=(P("row", None), P("row", None)),
        check_vma=False,
    )
```

time: 1980 us -> 1100 us (0.56)
  waiting for transfers between devices: 1260 us -> 480 us
  matrix products: 282 us -> 159 us
  blocking collectives: 45.8 us -> 94.9 us
  other arithmetic: 273 us -> 253 us
    psum x3, waiting for transfers between devices: 1030 us -> 86.2 us  [the longest x1 58.9 us: per_device(): return lax.psum((merged_part, rhs_part), 'task')]
    all_gather x1 -> x4, waiting for transfers between devices: 223 us -> 394 us  [the longest x1 170 us: per_device(): upper = lax.all_gather(mine, 'row', axis=1, tiled=True)]
    another operation x40 -> x26, matrix products: 148 us -> 31.2 us  [the longest x14 18.5 us: inverse_of(): return jax.scipy.linalg.solve_triangular(factor, identity, lower=True)]
    all_to_all x0 -> x1, blocking collectives: none -> 50.8 us  [leading_block(): lax.all_to_all(columns_block.reshape(parts, rows // parts, wide), 'row',...]
    another operation x37 -> x31, local copies, waits for them, and re-layouts: 49.3 us -> 19 us  [the longest x23 17.2 us: inverse_of(): return jax.scipy.linalg.solve_triangular(factor, identity, lower=True)]
    unnamed x62 -> x34, local copies, waits for them, and re-layouts: 40.9 us -> 22.7 us
    another operation x40 -> x41, other arithmetic: 226 us -> 236 us  [the longest x12 86.2 us: inverse_of(): return jax.scipy.linalg.solve_triangular(factor, identity, lower=True)]
    dot_general x4 -> x8, matrix products: 86.3 us -> 80.3 us  [product(): return jnp.dot(left, right, precision=lax.Precision.HIGHEST)]
  transfers between devices with their start and end apart: 4 -> 8, of which waited for: 4 -> 7; matrix products, arithmetic and copies ran while one was open for 2% -> 35% of each run, Pallas kernels for 0% -> 0%
where the time goes in v1:
time: 1100 us; the launch traced here: 1090 us
  waiting for transfers between devices  480 us (44%)
  other arithmetic  253 us (23%)
  matrix products  159 us (14%)
  blocking collectives  94.9 us (9%)
  local copies, waits for them, and re-layouts  77.6 us (7%)
  between operations  20.9 us (2%)
    all_gather x1, waiting for transfers between devices, per_device(): upper = lax.all_gather(mine, 'row', axis=1, tiled=True)  170 us
    all_gather x1, waiting for transfers between devices, per_device(): weights = lax.all_gather(adjusted_weights[0], 'row', axis=0, tiled=True)  143 us
    another operation x12, other arithmetic, inverse_of(): return jax.scipy.linalg.solve_triangular(factor, identity, lower=True)  86.2 us
    dot_general x8, matrix products, product(): return jnp.dot(left, right, precision=lax.Precision.HIGHEST)  80.3 us
    another operation x14, other arithmetic, per_device(): first_inverse = inverse_of(jnp.linalg.cholesky(corner[:rows, :rows]))  76.4 us
    another operation x15, other arithmetic, per_device(): second = jnp.linalg.cholesky(corner[rows:, rows:] - product(left, left.T))  73.5 us
    all_gather x1, waiting for transfers between devices, leading_block(): gathered = lax.all_gather(pieces, 'row', axis=1, tiled=True)  64.5 us
    psum x1, waiting for transfers between devices, per_device(): return lax.psum((merged_part, rhs_part), 'task')  58.9 us
  transfers between devices with their start and end apart: 8, of which 7 were waited for; matrix products, arithmetic and copies ran while one was open for 35% of the time, Pallas kernels for 0%

profile of v1, /device:TPU:0, one launch (start us, length us, event | category | flops | bytes accessed | tf_op | source)
XLA Modules:
  0.0 1092.9 jit_solution(17314033393186713697)
XLA Ops:
  7.2 1.6 dynamic-slice_bitcast_fusion
  8.8 3.9 gather_fusion
  13.3 44.1 %psum.35 = f32[]{:T(128)} all-reduce(f32[]{:T(128)} %reduce_sum.9), channel_id=1, replica_groups=mesh['task'=2,'row'=16] {'row'}, use_global_device_ids=true, to_apply=%region_1.2 | all-reduce | flops 1 | bytes 8 | tf_op jit(solution)/shard_map/psum | solution.py:45
  58.1 12.8 %fusion.6 = f32[448,7168]{1,0:T(8,128)} fusion(f32[1,448,7168]{2,1,0:T(8,128)} %param.5, s32[448]{0:T(512)S(1)} %iota_add_fusion, f32[]{:T(128)S(6)} %div.9), kind=kLoop, calls=%fused_computation.14 | loop fusion | flops 19267584 | bytes 25691908 | tf_op jit(solution)/shard_map/mul | solution.py:48
  70.8 2.7 slice.125
  73.6 16.4 %all-reduce.9.cloned.1.call-done = f32[448,896]{1,0:T(8,128)} async-done(((f32[448,896]{1,0:T(8,128)}), f32[448,896]{1,0:T(8,128)}) %all-reduce.9.cloned.1.call-update) | async-done | bytes 1605648 | tf_op jit(solution)/shard_map/psum | solution.py:50
  90.0 1.5 reshape.52
  91.5 50.8 %all_to_all.21 = f32[16,28,896]{2,1,0:T(8,128)S(1)} all-to-all(f32[16,28,896]{2,1,0:T(8,128)S(1)} %reshape.52), channel_id=1, replica_groups=mesh['task'=2,'row'=16] {'row'}, dimensions={0} | all-to-all | bytes 3211264 | tf_op jit(solution)/shard_map/all_to_all | solution.py:22
  145.0 64.5 %all-gather.6.cloned.1.call-done = f32[2,448,896]{2,0,1:T(2,128)} async-done(((f32[2,28,896]{2,0,1:T(2,128)}), f32[2,448,896]{2,0,1:T(2,128)}) %all-gather.6.cloned.1.call-update) | async-done | bytes 3211280 | tf_op jit(solution)/shard_map/all_gather | solution.py:25
  209.5 2.1 copy.21
  212.6 2.5 copy.41
  215.1 2.4 fusion.21
  218.6 11.7 %cholesky.292 = f32[128,128]{1,0:T(8,128)S(1)} custom-call(f32[128,128]{1,0:T(8,128)S(1)} %cholesky.440), custom_call_target="Cholesky" | custom-call | tf_op jit(solution)/shard_map/jit(cholesky)/cholesky | solution.py:52
  230.3 9.8 custom-call.29
  241.2 1.9 constant_dynamic-update-slice_fusion.5
  244.9 12.5 %cholesky.311 = f32[128,128]{1,0:T(8,128)S(1)} custom-call(f32[128,128]{1,0:T(8,128)} %cholesky.444), custom_call_target="Cholesky" | custom-call | tf_op jit(solution)/shard_map/jit(cholesky)/cholesky | solution.py:52
  258.1 10.9 custom-call.30
  269.9 1.6 convolution_subtract_fusion.10
  271.5 11.7 %cholesky.332 = f32[128,128]{1,0:T(8,128)S(1)} custom-call(f32[128,128]{1,0:T(8,128)S(1)} %cholesky.449), custom_call_target="Cholesky" | custom-call | tf_op jit(solution)/shard_map/jit(cholesky)/cholesky | solution.py:52
  283.8 9.8 custom-call.31
  295.6 5.8 cholesky.352
  309.2 9.3 while.4
  310.3 2.3 bitcast_dynamic-update-slice_fusion.4
  313.3 2.3 bitcast_dynamic-update-slice_fusion.4
  316.2 2.3 bitcast_dynamic-update-slice_fusion.4
  318.5 1.6 pad_maximum_fusion.1
  320.1 40.7 %custom-call.32 = f32[4,128,128]{1,2,0:T(8,128)} custom-call(f32[4,128,128]{2,1,0:T(8,128)} %pad_maximum_fusion.1), custom_call_target="InvertDiagBlocksLowerTriangular" | custom-call | tf_op jit(solution)/shard_map/jit(_solve_triangular)/triangular_solve | solution.py:15
  360.8 2.7 copy.42
  367.6 1.6 convolution_subtract_fusion.5
  370.4 1.8 convolution_subtract_fusion.4
  374.0 1.6 fusion.11
  376.6 1.6 convolution_subtract_fusion
  378.6 143.0 %all-gather.12.cloned.1.call-done = bf16[1,7168,2048]{2,1,0:T(8,128)(2,1)} async-done(((bf16[1,448,2048]{2,1,0:T(8,128)(2,1)}), bf16[1,7168,2048]{2,1,0:T(8,128)(2,1)}) %all-gather.12.cloned.1.call-update) | async-done | bytes 29360144 | tf_op jit(solution)/shard_map/all_gather | solution.py:41
  521.6 23.8 %fusion = f32[448,2048]{1,0:T(8,128)} fusion(bf16[1,7168,2048]{2,1,0:T(8,128)(2,1)} %all-gather.12.cloned.1.call-done, f32[448,7168]{1,0:T(8,128)} %fusion.6), kind=kOutput, calls=%fused_computation.5 | convolution fusion | flops 13162971136 | bytes 45875200 | tf_op jit(solution)/shard_map/dot_general | solution.py:69
  545.4 24.2 %fusion.8 = f32[448,2048]{1,0:T(8,128)} fusion(f32[448,2048]{1,0:T(8,128)} %fusion, bf16[1,7168,2048]{2,1,0:T(8,128)(2,1)} %all-gather.12.cloned.1.call-done, f32[448,7168]{1,0:T(8,128)} %fusion.6), kind=kOutput, calls=%fused_computation.19 | convolution fusion | flops 13160677376 | bytes 49545216 | tf_op jit(solution)/shard_map/dot_general | solution.py:67
  569.6 4.2 copy_bitcast_fusion
  573.8 4.5 all-to-all-start.1
  579.7 11.7 %cholesky.368 = f32[128,128]{1,0:T(8,128)S(1)} custom-call(f32[128,128]{1,0:T(8,128)S(1)} %cholesky.453), custom_call_target="Cholesky" | custom-call | tf_op jit(solution)/shard_map/jit(cholesky)/cholesky | solution.py:54
  591.6 9.8 custom-call.33
  603.8 11.7 %cholesky.387 = f32[128,128]{1,0:T(8,128)S(1)} custom-call(f32[128,128]{1,0:T(8,128)S(1)} %cholesky.457), custom_call_target="Cholesky" | custom-call | tf_op jit(solution)/shard_map/jit(cholesky)/cholesky | solution.py:54
  615.6 10.2 custom-call.34
  627.3 11.7 %cholesky.408 = f32[128,128]{1,0:T(8,128)S(1)} custom-call(f32[128,128]{1,0:T(8,128)S(1)} %cholesky.462), custom_call_target="Cholesky" | custom-call | tf_op jit(solution)/shard_map/jit(cholesky)/cholesky | solution.py:54
  639.0 9.8 custom-call.35
  650.0 5.8 cholesky.428
  661.8 8.5 while.5
  662.6 2.2 bitcast_dynamic-update-slice_fusion.5
  665.4 2.2 bitcast_dynamic-update-slice_fusion.5
  668.2 2.2 bitcast_dynamic-update-slice_fusion.5
  671.1 40.7 %custom-call.36 = f32[4,128,128]{1,2,0:T(8,128)} custom-call(f32[4,128,128]{2,1,0:T(8,128)} %pad_maximum_fusion.2), custom_call_target="InvertDiagBlocksLowerTriangular" | custom-call | tf_op jit(solution)/shard_map/jit(_solve_triangular)/triangular_solve | solution.py:15
  718.1 1.6 convolution_subtract_fusion.1
  720.8 1.6 fusion.84
  722.5 1.9 convolution_negate_fusion
  724.7 1.8 slice.130
  726.8 7.3 fusion.87
  735.5 10.9 %all-reduce.11.cloned.1.call-done = f32[896,128]{1,0:T(8,128)} async-done(((f32[896,128]{1,0:T(8,128)}), f32[896,128]{1,0:T(8,128)}) %all-reduce.11.cloned.1.call-update) | async-done | bytes 458768 | tf_op jit(solution)/shard_map/psum | solution.py:73
  746.4 4.8 fusion.88
  751.5 170.0 %all-gather.8.cloned.1.call-done = f32[448,7168]{0,1:T(8,128)} async-done(((f32[448,448]{0,1:T(8,128)}), f32[448,7168]{0,1:T(8,128)}) %all-gather.8.cloned.1.call-update) | async-done | bytes 12845072 | tf_op jit(solution)/shard_map/all_gather | solution.py:63
  921.5 14.6 %copy.33 = f32[448,7168]{1,0:T(8,128)} copy(f32[448,7168]{0,1:T(8,128)} %all-gather.8.cloned.1.call-done) | data formatting | bytes 25690112 | tf_op jit(solution)/shard_map/all_gather | solution.py:63
  936.2 51.1 %select_select_fusion = f32[448,7168]{1,0:T(8,128)} fusion(f32[448,7168]{1,0:T(8,128)} %copy.33, f32[448,7168]{1,0:T(8,128)} %fusion.6, f32[448,448]{1,0:T(8,128)S(1)} %fusion.87, f32[448,7168]{0,1:T(8,128)} %all-gather.8.cloned.1.call-done, pred[]{:T(512)S(6)} %eq.18, pred[]{:T(512)S(6)} %ge.6), kind=kOutput, calls=%fused_computation.15 | convolution fusion | flops 17273389056 | bytes 52183040 | tf_op jit(solution)/shard_map/dot_general | solution.py:10
  987.2 16.1 %all-gather.10.cloned.1.call-done = f32[448,2048]{1,0:T(8,128)} async-done(((f32[448,128]{1,0:T(8,128)}), f32[448,2048]{1,0:T(8,128)}) %all-gather.10.cloned.1.call-update) | async-done | bytes 3670032 | tf_op jit(solution)/shard_map/all_gather | solution.py:74
  1003.4 10.3 select_select_fusion.1
  1013.7 58.9 %all-reduce.13.cloned.1.call-done = (f32[448,7168]{1,0:T(8,128)}, f32[448,2048]{1,0:T(8,128)}) async-done(((f32[448,7168]{1,0:T(8,128)}, f32[448,2048]{1,0:T(8,128)}), (f32[448,7168]{1,0:T(8,128)}, f32[448,2048]{1,0:T(8,128)})) %all-reduce.13.cloned.1.call-update) | async-done | bytes 16515088 | tf_op jit(solution)/shard_map/psum | solution.py:84
  1072.6 11.2 %copy.79 = f32[448,7168]{1,0:T(8,128)} copy(f32[448,7168]{1,0:T(8,128)} %get-tuple-element.162) | data formatting | bytes 25690112
  1083.7 1.8 copy.80
  (126 shorter events, 50.1 us)
Async XLA Ops:
  7.2 82.8 %all-reduce.9.cloned.1.call-start = ((), (), s32[]{:S(2)}) async-start(), calls=%async_computation.2 | async-start | bytes 3211264 | tf_op jit(solution)/shard_map/psum | solution.py:50
  73.5 135.9 %all-gather.6.cloned.1.call-start = ((), (), s32[]{:S(2)}) async-start(), calls=%async_computation.3 | async-start | bytes 3411968 | tf_op jit(solution)/shard_map/all_gather | solution.py:25
  143.1 378.5 %all-gather.12.cloned.1.call-start = ((), (), s32[]{:S(2)}) async-start(), calls=%async_computation.7 | async-start | bytes 31195136 | tf_op jit(solution)/shard_map/all_gather | solution.py:41
  217.6 1.0 copy-start.13
  308.2 1.0 copy-start.12
  364.9 11.7 %copy-start.7 = (f32[448,448]{0,1:T(8,128)S(1)}, f32[448,448]{0,1:T(8,128)}, u32[]{:S(2)}) copy-start(f32[448,448]{0,1:T(8,128)} %copy.42) | copy-start | bytes 2408452
  367.5 5.7 copy-start.3
  370.4 2.9 copy-start.5
  373.3 0.7 copy-start.9
  375.6 1.0 copy-start
  573.8 150.9 %all-to-all-start.1 = ((f32[448,16,128]{2,0,1:T(8,128)}), f32[448,16,128]{2,0,1:T(8,128)}, u32[]{:S(2)}, u32[]{:S(2)}) async-start(f32[448,16,128]{2,0,1:T(8,128)} %copy_bitcast_fusion), calls=%async_computation.1 | async-start | bytes 7340032 | tf_op jit(solution)/shard_map/all_to_all | solution.py:71
  578.3 168.1 %all-reduce.11.cloned.1.call-start = ((), (), s32[]{:S(2)}) async-start(), calls=%async_computation.5 | async-start | bytes 917504 | tf_op jit(solution)/shard_map/psum | solution.py:73
  578.8 0.9 copy-start.14
  591.4 120.4 %copy-start.4 = (f32[128,448]{0,1:T(8,128)S(1)}, f32[128,448]{0,1:T(8,128)}, u32[]{:S(2)}) copy-start(f32[128,448]{0,1:T(8,128)} %copy-done.3) | copy-start | bytes 688132
  591.4 120.4 %copy-start.6 = (f32[128,448]{0,1:T(8,128)S(1)}, f32[128,448]{0,1:T(8,128)}, u32[]{:S(2)}) copy-start(f32[128,448]{0,1:T(8,128)} %copy-done.5) | copy-start | bytes 688132
  591.4 120.4 %copy-start.10 = (f32[64,448]{0,1:T(8,128)S(1)}, f32[64,448]{0,1:T(8,128)}, u32[]{:S(2)}) copy-start(f32[64,448]{0,1:T(8,128)} %copy-done.9) | copy-start | bytes 344068
  603.8 108.1 %copy-start.2 = (f32[448,448]{0,1:T(8,128)S(1)}, f32[448,448]{0,1:T(8,128)}, u32[]{:S(2)}) copy-start(f32[448,448]{0,1:T(8,128)} %fusion.22) | copy-start | bytes 2408452
  660.9 0.9 copy-start.11
  670.4 50.5 %copy-start.1 = (f32[448,448]{1,0:T(8,128)S(1)}, f32[448,448]{1,0:T(8,128)}, u32[]{:S(2)}) copy-start(f32[448,448]{1,0:T(8,128)} %copy-done) | copy-start | bytes 2408452
  726.6 195.0 %all-gather.8.cloned.1.call-start = ((), (), s32[]{:S(2)}) async-start(), calls=%async_computation.4 | async-start | bytes 15597568 | tf_op jit(solution)/shard_map/all_gather | solution.py:63
  735.5 267.9 %all-gather.10.cloned.1.call-start = ((), (), s32[]{:S(2)}) async-start(), calls=%async_computation.6 | async-start | bytes 3899392 | tf_op jit(solution)/shard_map/all_gather | solution.py:74
  751.2 321.3 %all-reduce.13.cloned.1.call-start = ((), (), s32[]{:S(2)}) async-start(), calls=%async_computation.8 | async-start | bytes 33030144 | tf_op jit(solution)/shard_map/psum | solution.py:84
  1072.6 11.2 %copy-start.8 = (f32[448,2048]{1,0:T(8,128)S(1)}, f32[448,2048]{1,0:T(8,128)}, u32[]{:S(2)}) copy-start(f32[448,2048]{1,0:T(8,128)} %get-tuple-element.163) | copy-start | bytes 11010052
Sparse Core Ops, SparseCore 0:
  73.7 16.2 all-reduce.8
  143.2 66.1 all-gather.5
  212.2 309.3 all-gather.11
  726.7 19.6 all-reduce.10
  749.0 172.4 all-gather.7
  924.1 79.2 all-gather.9
  1013.8 58.6 all-reduce.12
